TPU v7x, 32 devices: a whole 2x2x4 slice. The times are simulated.
32 devices in a mesh: pb: 4 (over x, core), ka: 8 (over z, y).
Axes of the slice: x: 2, y: 2, z: 4, core: 2. Of those that a mesh axis runs over, the one named last changes fastest.
Arguments:
- queries: bfloat16 [4096, 1024], P(('pb', 'ka')), may hold values from -6 to 6
- key_rows: bfloat16 [4096, 128], P(('pb', 'ka')), may hold values from -6 to 6
- value_rows: bfloat16 [4096, 128], P(('pb', 'ka')), may hold values from -6 to 6
- forward_out: bfloat16 [4096, 1024], P(('pb', 'ka')), may hold values from -6 to 6
- out_grad: bfloat16 [4096, 1024], P(('pb', 'ka')), may hold values from -4 to 4
- logsumexp: float32 [8, 4096], P(None, ('pb', 'ka')), may hold values from 3 to 7
- position: int32 [4096], P(('pb', 'ka')), may hold values from 0 to 4095, as said below
- segment: int32 [4096], P(('pb', 'ka')), may hold values from 0 to 7, as said below
Outputs:
- query_grad: bfloat16 [4096, 1024], P(('pb', 'ka'))
- key_grad: bfloat16 [4096, 128], P(('pb', 'ka'))
- value_grad: bfloat16 [4096, 128], P(('pb', 'ka'))
Inputs may be any that keep to these rules, and one draw needn't show every extreme that they name: `position`: a permutation of 0 to 4095; each aligned run of 128 rows holds 128 consecutive positions in increasing order. `segment`: the document of the row's position; each document is a nonempty run of consecutive positions, numbered in the order of positions, 8 documents in all.
All inputs are finite; a program needn't handle non-finite values.
Results may differ from a plain program's by a relative error of at most 0.0051.
Values may be sent and summed in bfloat16 or wider, within the bound.
No kernel may reach another device: no remote copies, remote signals or barrier semaphores. Data moves between devices by JAX's collectives and lax.ppermute only.
A program may use at most 64 MiB of HBM per device.

v0:
```python
import jax
import jax.numpy as jnp
from jax import lax
from jax.sharding import PartitionSpec as P


def tile_terms(query_tile, grad_tile, lse_tile, delta_tile, key_tile, value_tile, visible):
    tile_rows = query_tile.shape[0]
    head_width = key_tile.shape[1]
    head_count = query_tile.shape[1] // head_width
    score_scale = head_width ** (-0.5)
    query_heads = query_tile.reshape(tile_rows, head_count, head_width)
    grad_heads = grad_tile.reshape(tile_rows, head_count, head_width)
    scores = (
        jnp.einsum("qhd,kd->hqk", query_heads, key_tile, preferred_element_type=jnp.float32)
        * score_scale
    )
    weights = jnp.where(visible[None], jnp.exp(scores - lse_tile[:, :, None]), 0.0)
    rounded = weights.astype(jnp.bfloat16)
    value_term = jnp.einsum("hqk,qhd->kd", rounded, grad_heads, preferred_element_type=jnp.float32)
    grad_scores = jnp.einsum(
        "qhd,kd->hqk", grad_heads, value_tile, preferred_element_type=jnp.float32
    )
    score_grads = (weights * (grad_scores - delta_tile[:, :, None])).astype(jnp.bfloat16)
    query_term = jnp.einsum(
        "hqk,kd->qhd", score_grads, key_tile, preferred_element_type=jnp.float32
    ).reshape(tile_rows, head_count * head_width)
    key_term = jnp.einsum(
        "hqk,qhd->kd", score_grads, query_heads, preferred_element_type=jnp.float32
    )
    return (query_term, key_term, value_term)


def all_grads(
    query_block,
    grad_block,
    lse_block,
    delta_block,
    query_place,
    query_doc,
    key_block,
    value_block,
    key_place,
    key_doc,
):
    query_total = query_block.shape[0]
    key_total = key_block.shape[0]
    head_width = key_block.shape[1]
    row_width = query_block.shape[1]
    query_step = min(512, query_total)
    key_step = min(256, key_total)

    def over_queries(query_index, loop_state):
        query_out, key_out, value_out = loop_state
        query_start = query_index * query_step
        query_tile = lax.dynamic_slice_in_dim(query_block, query_start, query_step, 0)
        grad_tile = lax.dynamic_slice_in_dim(grad_block, query_start, query_step, 0)
        lse_tile = lax.dynamic_slice_in_dim(lse_block, query_start, query_step, 1)
        delta_tile = lax.dynamic_slice_in_dim(delta_block, query_start, query_step, 1)
        place_tile = lax.dynamic_slice_in_dim(query_place, query_start, query_step, 0)
        doc_tile = lax.dynamic_slice_in_dim(query_doc, query_start, query_step, 0)

        def over_keys(key_index, inner_state):
            query_acc, key_out, value_out = inner_state
            key_start = key_index * key_step
            key_tile = lax.dynamic_slice_in_dim(key_block, key_start, key_step, 0)
            value_tile = lax.dynamic_slice_in_dim(value_block, key_start, key_step, 0)
            key_place_tile = lax.dynamic_slice_in_dim(key_place, key_start, key_step, 0)
            key_doc_tile = lax.dynamic_slice_in_dim(key_doc, key_start, key_step, 0)
            visible = (key_place_tile[None, :] <= place_tile[:, None]) & (
                key_doc_tile[None, :] == doc_tile[:, None]
            )
            operands = (query_tile, grad_tile, lse_tile, delta_tile, key_tile, value_tile, visible)
            query_term, key_term, value_term = tile_terms(*operands)
            key_slab = lax.dynamic_slice_in_dim(key_out, key_start, key_step, 0)
            key_out = lax.dynamic_update_slice_in_dim(key_out, key_slab + key_term, key_start, 0)
            value_slab = lax.dynamic_slice_in_dim(value_out, key_start, key_step, 0)
            value_out = lax.dynamic_update_slice_in_dim(
                value_out, value_slab + value_term, key_start, 0
            )
            return (query_acc + query_term, key_out, value_out)

        inner_start = (jnp.zeros((query_step, row_width), jnp.float32), key_out, value_out)
        query_acc, key_out, value_out = lax.fori_loop(
            0, key_total // key_step, over_keys, inner_start
        )
        query_out = lax.dynamic_update_slice_in_dim(query_out, query_acc, query_start, 0)
        return (query_out, key_out, value_out)

    starting = (
        jnp.zeros((query_total, row_width), jnp.float32),
        jnp.zeros((key_total, head_width), jnp.float32),
        jnp.zeros((key_total, head_width), jnp.float32),
    )
    return lax.fori_loop(0, query_total // query_step, over_queries, starting)


def body(queries, key_rows, value_rows, forward_out, out_grad, logsumexp, position, segment):
    head_width = key_rows.shape[1]
    head_count = queries.shape[1] // head_width
    local_rows = queries.shape[0]
    score_scale = head_width ** (-0.5)
    delta_rows = jnp.sum(
        (out_grad.astype(jnp.float32) * forward_out.astype(jnp.float32)).reshape(
            local_rows, head_count, head_width
        ),
        axis=2,
    ).T
    query_block, grad_block, query_place, query_doc = (
        lax.all_gather(queries, "ka", axis=0, tiled=True),
        lax.all_gather(out_grad, "ka", axis=0, tiled=True),
        lax.all_gather(position, "ka", axis=0, tiled=True),
        lax.all_gather(segment, "ka", axis=0, tiled=True),
    )
    lse_block, delta_block = (
        lax.all_gather(logsumexp, "ka", axis=1, tiled=True),
        lax.all_gather(delta_rows, "ka", axis=1, tiled=True),
    )
    key_block, value_block, key_place, key_doc = (
        lax.all_gather(key_rows, "pb", axis=0, tiled=True),
        lax.all_gather(value_rows, "pb", axis=0, tiled=True),
        lax.all_gather(position, "pb", axis=0, tiled=True),
        lax.all_gather(segment, "pb", axis=0, tiled=True),
    )
    query_sum, key_sum, value_sum = all_grads(
        query_block,
        grad_block,
        lse_block,
        delta_block,
        query_place,
        query_doc,
        key_block,
        value_block,
        key_place,
        key_doc,
    )
    query_grad = lax.psum_scatter(query_sum * score_scale, "ka", scatter_dimension=0, tiled=True)
    key_grad, value_grad = (
        lax.psum_scatter(key_sum * score_scale, "pb", scatter_dimension=0, tiled=True),
        lax.psum_scatter(value_sum, "pb", scatter_dimension=0, tiled=True),
    )
    return (
        query_grad.astype(jnp.bfloat16),
        key_grad.astype(jnp.bfloat16),
        value_grad.astype(jnp.bfloat16),
    )


def solution(mesh):
    placed = (
        P(("pb", "ka"), None),
        P(("pb", "ka"), None),
        P(("pb", "ka"), None),
        P(("pb", "ka"), None),
        P(("pb", "ka"), None),
        P(None, ("pb", "ka")),
        P(("pb", "ka")),
        P(("pb", "ka")),
    )
    return jax.shard_map(
        body,
        mesh=mesh,
        in_specs=placed,
        out_specs=(P(("pb", "ka"), None), P(("pb", "ka"), None), P(("pb", "ka"), None)),
        check_vma=False,
    )
```

profile of v0, /device:TPU:0, one launch (start us, length us, event | category | flops | bytes accessed | tf_op | source)
XLA Modules:
  0.0 322.1 jit_solution(15213432203039361931)
XLA Ops:
  7.3 0.7 all-gather.7.cloned.1.call-update
  8.0 0.7 all-gather.9.cloned.1.call-update
  8.7 1.1 multiply_bitcast_fusion
  10.2 33.8 %all_gather.35 = f32[8,1024]{0,1:T(8,128)S(1)} all-gather(f32[8,128]{0,1:T(8,128)S(1)} %bitcast.125), channel_id=1, replica_groups=mesh['pb'=4,'ka'=8] {'ka'}, dimensions={1}, use_global_device_ids=true | all-gather | bytes 36864 | tf_op jit(solution)/shard_map/all_gather | solution.py:117
  44.1 5.1 %all-gather.2 = s32[4,1,128]{2,1,0:T(1,128)S(1)} all-gather(s32[1,1,128]{2,1,0:T(1,128)S(1)} %bitcast.128), channel_id=1, replica_groups=mesh['pb'=4,'ka'=8] {'pb'}, dimensions={0}, use_global_device_ids=true | all-gather | bytes 2560 | tf_op jit(solution)/shard_map/all_gather | solution.py:122
  49.2 5.0 %all-gather.3 = s32[4,1,128]{2,1,0:T(1,128)S(1)} all-gather(s32[1,1,128]{2,1,0:T(1,128)S(1)} %bitcast.130), channel_id=1, replica_groups=mesh['pb'=4,'ka'=8] {'pb'}, dimensions={0}, use_global_device_ids=true | all-gather | bytes 2560 | tf_op jit(solution)/shard_map/all_gather | solution.py:123
  54.2 20.7 %all-gather = s32[8,1,128]{2,1,0:T(1,128)S(1)} all-gather(s32[1,1,128]{2,1,0:T(1,128)S(1)} %bitcast.129), channel_id=1, replica_groups=mesh['pb'=4,'ka'=8] {'ka'}, dimensions={0}, use_global_device_ids=true | all-gather | bytes 4608 | tf_op jit(solution)/shard_map/all_gather | solution.py:112
  75.0 16.3 %all-gather.1 = s32[8,1,128]{2,1,0:T(1,128)S(1)} all-gather(s32[1,1,128]{2,1,0:T(1,128)S(1)} %bitcast.131), channel_id=1, replica_groups=mesh['pb'=4,'ka'=8] {'ka'}, dimensions={0}, use_global_device_ids=true | all-gather | bytes 4608 | tf_op jit(solution)/shard_map/all_gather | solution.py:113
  91.3 31.1 %all_gather.34 = f32[8,1024]{1,0:T(8,128)S(1)} all-gather(f32[8,128]{1,0:T(8,128)S(1)} %copy-done.17), channel_id=1, replica_groups=mesh['pb'=4,'ka'=8] {'ka'}, dimensions={1}, use_global_device_ids=true | all-gather | bytes 36864 | tf_op jit(solution)/shard_map/all_gather | solution.py:116
  122.3 5.4 %all_gather.36 = bf16[512,128]{1,0:T(8,128)(2,1)S(1)} all-gather(bf16[128,128]{1,0:T(8,128)(2,1)S(1)} %copy-done.15), channel_id=1, replica_groups=mesh['pb'=4,'ka'=8] {'pb'}, dimensions={0}, use_global_device_ids=true | all-gather | bytes 163840 | tf_op jit(solution)/shard_map/all_gather | solution.py:120
  127.7 5.9 %all_gather.39 = bf16[512,128]{1,0:T(8,128)(2,1)} all-gather(bf16[128,128]{1,0:T(8,128)(2,1)S(1)} %copy-done.16), channel_id=1, replica_groups=mesh['pb'=4,'ka'=8] {'pb'}, dimensions={0}, use_global_device_ids=true | all-gather | bytes 163840 | tf_op jit(solution)/shard_map/all_gather | solution.py:121
  133.6 0.7 broadcast.67
  134.3 2.5 broadcast_in_dim.49.clone
  136.9 42.4 %while.52 = (s32[]{:T(128)}, f32[1024,1024]{1,0:T(8,128)}, f32[512,128]{1,0:T(8,128)}, f32[512,128]{1,0:T(8,128)S(1)}, s32[1024]{0:T(1024)S(1)}, /*index=5*/s32[...) while((s32[]{:T(128)}, f32[1024,1024]{1,0:T(8,128)}, ...), condition=%wide.region_4.5_spmd, body=%wide.region_1.4_spmd.sunk | while | flops 1354170368 | bytes 52825124 | solution.py:95
  138.3 2.8 constant_dynamic-slice_fusion.6
  141.0 11.9 %while.53 = (s32[]{:T(128)}, f32[512,1024]{0,1:T(8,128)S(1)}, f32[512,128]{1,0:T(8,128)}, f32[512,128]{1,0:T(8,128)S(1)}, bf16[512,128]{1,0:T(8,128)(2,1)S(1)}, ...) while((s32[]{:T(128)}, f32[512,1024]{0,1:T(8,128)S(1)}, ...), condition=%wide.region_3.3_spmd.clone, body=%wide.region_2.2_spmd.clone.sunk | while | flops 1354170368 | bytes 39578024 | solution.py:84
  141.4 0.7 fusion.79
  142.3 1.1 fusion.83
  143.5 1.6 fusion.80
  145.1 0.8 fusion.82
  146.3 0.6 bitcast_add_fusion.2
  147.3 0.7 fusion.79
  148.2 1.1 fusion.83
  149.4 1.6 fusion.80
  151.0 0.8 fusion.82
  152.9 1.9 copy.56
  154.8 3.2 constant_dynamic-update-slice_fusion.2
  159.4 2.8 constant_dynamic-slice_fusion.6
  162.2 11.9 %while.53 = (s32[]{:T(128)}, f32[512,1024]{0,1:T(8,128)S(1)}, f32[512,128]{1,0:T(8,128)}, f32[512,128]{1,0:T(8,128)S(1)}, bf16[512,128]{1,0:T(8,128)(2,1)S(1)}, ...) while((s32[]{:T(128)}, f32[512,1024]{0,1:T(8,128)S(1)}, ...), condition=%wide.region_3.3_spmd.clone, body=%wide.region_2.2_spmd.clone.sunk | while | flops 1354170368 | bytes 39578024 | solution.py:84
  162.6 0.7 fusion.79
  163.5 1.1 fusion.83
  164.6 1.6 fusion.80
  166.3 0.8 fusion.82
  168.5 0.7 fusion.79
  169.4 1.1 fusion.83
  170.6 1.6 fusion.80
  172.2 0.8 fusion.82
  174.1 1.9 copy.56
  176.0 3.2 %constant_dynamic-update-slice_fusion.2 = f32[1024,1024]{1,0:T(8,128)} fusion(f32[1024,1024]{1,0:T(8,128)} %get-tuple-element.913, f32[512,1024]{1,0:T(8,128)} %copy.56, s32[]{:T(128)S(6)} %select_n.53), kind=kLoop, calls=%fused_computation.38.clone.1 | loop fusion | bytes 4194308 | tf_op jit(solution)/shard_map/while/body/eval_jaxpr/dynamic_update_slice | solution.py:87
  179.3 0.7 copy-done.1
  180.1 1.7 broadcast_multiply_fusion.1
  181.8 5.1 %broadcast_multiply_fusion = f32[1024,1024]{1,0:T(8,128)} fusion(f32[1024,1024]{1,0:T(8,128)} %get-tuple-element.501), kind=kLoop, calls=%fused_computation.43 | loop fusion | flops 1048576 | bytes 8388608 | tf_op jit(solution)/shard_map/mul | solution.py:137
  186.9 12.1 %reduce-scatter.8.cloned.1.call-done = f32[128,128]{1,0:T(8,128)} async-done(((f32[512,128]{1,0:T(8,128)}), f32[128,128]{1,0:T(8,128)}) %reduce-scatter.8.cloned.1.call-update) | async-done | bytes 65552 | tf_op jit(solution)/shard_map/reduce_scatter | solution.py:140
  199.0 1.5 convert_element_type.33
  200.5 21.5 %reduce-scatter.6.cloned.1.call-done = f32[128,128]{1,0:T(8,128)} async-done(((f32[512,128]{1,0:T(8,128)}), f32[128,128]{1,0:T(8,128)}) %reduce-scatter.6.cloned.1.call-update) | async-done | bytes 65552 | tf_op jit(solution)/shard_map/reduce_scatter | solution.py:139
  222.0 1.5 convert_element_type.32
  223.4 90.3 %reduce-scatter.4.cloned.1.call-done = f32[128,1024]{1,0:T(8,128)} async-done(((f32[1024,1024]{1,0:T(8,128)}), f32[128,1024]{1,0:T(8,128)}) %reduce-scatter.4.cloned.1.call-update) | async-done | bytes 524304 | tf_op jit(solution)/shard_map/reduce_scatter | solution.py:137
  313.8 1.8 convert_element_type.31
  (132 shorter events, 9.2 us)
Async XLA Ops:
  7.2 36.9 %copy-start.18 = (s32[128]{0:T(128)S(1)}, s32[128]{0:T(128)}, u32[]{:S(2)}) copy-start(s32[128]{0:T(128)} %param.18) | copy-start | bytes 1540
  7.2 42.0 %copy-start.19 = (s32[128]{0:T(128)S(1)}, s32[128]{0:T(128)}, u32[]{:S(2)}) copy-start(s32[128]{0:T(128)} %param.19) | copy-start | bytes 1540
  7.2 84.1 %copy-start.17 = (f32[8,128]{1,0:T(8,128)S(1)}, f32[8,128]{1,0:T(8,128)}, u32[]{:S(2)}) copy-start(f32[8,128]{1,0:T(8,128)} %param.17) | copy-start | bytes 12292
  7.2 115.1 %copy-start.15 = (bf16[128,128]{1,0:T(8,128)(2,1)S(1)}, bf16[128,128]{1,0:T(8,128)(2,1)}, u32[]{:S(2)}) copy-start(bf16[128,128]{1,0:T(8,128)(2,1)} %param.13) | copy-start | bytes 98308
  7.2 120.5 %copy-start.16 = (bf16[128,128]{1,0:T(8,128)(2,1)S(1)}, bf16[128,128]{1,0:T(8,128)(2,1)}, u32[]{:S(2)}) copy-start(bf16[128,128]{1,0:T(8,128)(2,1)} %param.14) | copy-start | bytes 98308
  7.2 126.4 %all-gather.7.cloned.1.call-start = ((), (), s32[]{:S(2)}) async-start(), calls=%async_computation.3 | async-start | bytes 2359296 | tf_op jit(solution)/shard_map/all_gather | solution.py:110
  8.0 125.6 %all-gather.9.cloned.1.call-start = ((), (), s32[]{:S(2)}) async-start(), calls=%async_computation.4 | async-start | bytes 2359296 | tf_op jit(solution)/shard_map/all_gather | solution.py:111
  8.7 190.3 %reduce-scatter.8.cloned.1.call-start = ((), (), s32[]{:S(2)}) async-start(), calls=%async_computation.7 | async-start | bytes 327680 | tf_op jit(solution)/shard_map/reduce_scatter | solution.py:140
  136.9 1.3 copy-start.6
  136.9 1.3 copy-start.8
  136.9 1.3 copy-start.11
  141.0 1.2 copy-start
  141.0 1.2 copy-start.5
  142.3 1.2 copy-start.4
  142.3 1.2 copy-start.10
  143.4 1.6 copy-start.2
  145.8 1.1 copy-start.3
  147.0 1.2 copy-start
  147.0 1.2 copy-start.5
  148.2 1.2 copy-start.4
  148.2 1.2 copy-start.10
  149.4 1.6 copy-start.2
  151.8 1.1 copy-start.3
  152.9 5.1 %copy-start.14 = (s32[1024]{0:T(1024)S(1)}, s32[1024]{0:T(1024)}, u32[]{:S(2)}) copy-start(s32[1024]{0:T(1024)} %copy-done.13) | copy-start | bytes 12292 | tf_op jit(solution)/shard_map/while
  154.8 3.2 copy-start.7
  154.8 3.2 copy-start.9
  154.8 3.2 copy-start.12
  158.1 1.3 copy-start.6
  158.1 1.3 copy-start.8
  158.1 1.3 copy-start.11
  162.2 1.2 copy-start
  162.2 1.2 copy-start.5
  163.4 1.2 copy-start.4
  163.5 1.2 copy-start.10
  164.6 1.6 copy-start.2
  167.0 1.1 copy-start.3
  168.2 1.2 copy-start
  168.2 1.2 copy-start.5
  169.4 1.2 copy-start.4
  169.4 1.2 copy-start.10
  170.6 1.6 copy-start.2
  173.0 1.1 copy-start.3
  174.1 5.2 %copy-start.14 = (s32[1024]{0:T(1024)S(1)}, s32[1024]{0:T(1024)}, u32[]{:S(2)}) copy-start(s32[1024]{0:T(1024)} %copy-done.13) | copy-start | bytes 12292 | tf_op jit(solution)/shard_map/while
  176.0 3.3 %copy-start.7 = (f32[8,1024]{1,0:T(8,128)S(1)}, f32[8,1024]{1,0:T(8,128)}, u32[]{:S(2)}) copy-start(f32[8,1024]{1,0:T(8,128)} %copy-done.6) | copy-start | bytes 98308 | tf_op jit(solution)/shard_map/while
  176.0 3.3 %copy-start.9 = (f32[8,1024]{1,0:T(8,128)S(1)}, f32[8,1024]{1,0:T(8,128)}, u32[]{:S(2)}) copy-start(f32[8,1024]{1,0:T(8,128)} %copy-done.8) | copy-start | bytes 98308 | tf_op jit(solution)/shard_map/while
  176.0 3.3 %copy-start.12 = (s32[1024]{0:T(1024)S(1)}, s32[1024]{0:T(1024)}, u32[]{:S(2)}) copy-start(s32[1024]{0:T(1024)} %copy-done.11) | copy-start | bytes 12292 | tf_op jit(solution)/shard_map/while
  180.0 41.9 %reduce-scatter.6.cloned.1.call-start = ((), (), s32[]{:S(2)}) async-start(), calls=%async_computation.6 | async-start | bytes 327680 | tf_op jit(solution)/shard_map/reduce_scatter | solution.py:139
  181.8 132.0 %reduce-scatter.4.cloned.1.call-start = ((), (), s32[]{:S(2)}) async-start(), calls=%async_computation.5 | async-start | bytes 4718592 | tf_op jit(solution)/shard_map/reduce_scatter | solution.py:137
  (3 other events, 1.9 us)
Sparse Core Ops, SparseCore 0:
  10.2 53.5 all-gather.6
  65.9 48.1 all-gather.8
  180.1 18.8 reduce-scatter.7
  201.9 20.0 reduce-scatter.5
  225.4 88.2 reduce-scatter.3
where the time goes:
time: 323 us; the launch traced here: 322 us
  waiting for transfers between devices  125 us (39%)
  blocking collectives  123 us (38%)
  local copies, waits for them, and re-layouts  24.1 us (7%)
  matrix products  18.8 us (6%)
  other arithmetic  15.9 us (5%)
  between operations  13.9 us (4%)
    reduce_scatter x1, waiting for transfers between devices, body(): lax.psum_scatter(query_sum * score_scale, 'ka', scatter_dimension=0, tile...  90.3 us
    all_gather x1, blocking collectives, body(): lax.all_gather(delta_rows, 'ka', axis=1, tiled=True)  33.8 us
    all_gather x1, blocking collectives, body(): lax.all_gather(logsumexp, 'ka', axis=1, tiled=True)  31.1 us
    reduce_scatter x1, waiting for transfers between devices, body(): lax.psum_scatter(key_sum * score_scale, 'pb', scatter_dimension=0, tiled=...  21.5 us
    all_gather x1, blocking collectives, body(): lax.all_gather(position, 'ka', axis=0, tiled=True)  20.7 us
    all_gather x1, blocking collectives, body(): lax.all_gather(segment, 'ka', axis=0, tiled=True)  16.3 us
    reduce_scatter x1, waiting for transfers between devices, body(): lax.psum_scatter(value_sum, 'pb', scatter_dimension=0, tiled=True)  12.1 us
    dynamic_update_slice x4, local copies, waits for them, and re-layouts, over_queries(): lax.dynamic_update_slice_in_dim(query_out, query_acc, query_start, 0)  10.2 us
  transfers between devices with their start and end apart: 5, of which 3 were waited for; matrix products, arithmetic and copies ran while one was open for 3% of the time, Pallas kernels for 0%

commit v1 on v0

--- a/solution.py
+++ b/solution.py
@@ -1,7 +1,25 @@
+import functools
 import jax
 import jax.numpy as jnp
 from jax import lax
 from jax.sharding import PartitionSpec as P
+
+
+def group_detail(own_rows, ndim_at):
+    z_new = jax.lax.axis_size("ka")
+    state_now = jax.lax.axis_index("ka")
+    shaped, high = (z_new, state_now)
+    upper, latest = (own_rows, 1)
+    while latest < shaped:
+        outer = jax.lax.ppermute(upper, "ka", [(m, m ^ latest) for m in range(shaped)])
+        before = jnp.concatenate([upper, outer], axis=ndim_at)
+        later = jnp.concatenate([outer, upper], axis=ndim_at)
+        upper = jnp.where(high & latest == 0, before, later)
+        latest = 2 * latest
+    return upper
+
+
+draw_notes = functools.partial(group_detail, ndim_at=1)
 
 
 def tile_terms(query_tile, grad_tile, lse_tile, delta_tile, key_tile, value_tile, visible):
@@ -113,7 +131,7 @@
         lax.all_gather(segment, "ka", axis=0, tiled=True),
     )
     lse_block, delta_block = (
-        lax.all_gather(logsumexp, "ka", axis=1, tiled=True),
+        draw_notes(logsumexp),
         lax.all_gather(delta_rows, "ka", axis=1, tiled=True),
     )
     key_block, value_block, key_place, key_doc = (

time: 323 us -> 307 us (0.950)
  blocking collectives: 123 us -> 90.1 us
  waiting for transfers between devices: 125 us -> 135 us
  starting transfers between devices: 0.2 us -> 7.49 us
    all_gather x1 -> x0, blocking collectives: 31.1 us -> none  [body(): lax.all_gather(logsumexp, 'ka', axis=1, tiled=True)]
    all_gather x1, waiting for transfers between devices: 0.01 us -> 9.54 us  [body(): lax.all_gather(out_grad, 'ka', axis=0, tiled=True)]
    ppermute x0 -> x3, starting transfers between devices: none -> 7.29 us  [group_detail(): jax.lax.ppermute(upper, 'ka', [(m, m ^ latest) for m in range(shaped)])]
    all_gather x1, blocking collectives: 20.7 us -> 17 us  [body(): lax.all_gather(position, 'ka', axis=0, tiled=True)]
  transfers between devices with their start and end apart: 5 -> 8, of which waited for: 3 -> 4; matrix products, arithmetic and copies ran while one was open for 3% -> 4% of each run, Pallas kernels for 0% -> 0%
where the time goes in v1:
time: 307 us; the launch traced here: 306 us
  waiting for transfers between devices  135 us (44%)
  blocking collectives  90.1 us (29%)
  local copies, waits for them, and re-layouts  24.1 us (8%)
  matrix products  18.8 us (6%)
  other arithmetic  16.7 us (5%)
  between operations  13.9 us (5%)
  starting transfers between devices  7.49 us (2%)
    reduce_scatter x1, waiting for transfers between devices, body(): lax.psum_scatter(query_sum * score_scale, 'ka', scatter_dimension=0, tile...  90.4 us
    all_gather x1, blocking collectives, body(): lax.all_gather(delta_rows, 'ka', axis=1, tiled=True)  32.6 us
    reduce_scatter x1, waiting for transfers between devices, body(): lax.psum_scatter(key_sum * score_scale, 'pb', scatter_dimension=0, tiled=...  21.5 us
    all_gather x1, blocking collectives, body(): lax.all_gather(segment, 'ka', axis=0, tiled=True)  17.9 us
    all_gather x1, blocking collectives, body(): lax.all_gather(position, 'ka', axis=0, tiled=True)  17 us
    reduce_scatter x1, waiting for transfers between devices, body(): lax.psum_scatter(value_sum, 'pb', scatter_dimension=0, tiled=True)  11.8 us
    dynamic_update_slice x4, local copies, waits for them, and re-layouts, over_queries(): lax.dynamic_update_slice_in_dim(query_out, query_acc, query_start, 0)  10.2 us
    all_gather x1, waiting for transfers between devices, body(): lax.all_gather(out_grad, 'ka', axis=0, tiled=True)  9.54 us
  transfers between devices with their start and end apart: 8, of which 4 were waited for; matrix products, arithmetic and copies ran while one was open for 4% of the time, Pallas kernels for 0%

profile of v1, /device:TPU:0, one launch (start us, length us, event | category | flops | bytes accessed | tf_op | source)
XLA Modules:
  0.0 306.4 jit_solution(12599970486847328840)
XLA Ops:
  8.7 3.1 collective-permute-start
  11.8 1.1 multiply_bitcast_fusion
  12.9 5.6 %all_gather.32 = bf16[512,128]{1,0:T(8,128)(2,1)S(1)} all-gather(bf16[128,128]{1,0:T(8,128)(2,1)} %param.13), channel_id=1, replica_groups=mesh['pb'=4,'ka'=8] {'pb'}, dimensions={0}, use_global_device_ids=true | all-gather | bytes 163840 | tf_op jit(solution)/shard_map/all_gather | solution.py:138
  18.5 0.8 maximum_select_fusion.2
  19.3 1.6 collective-permute-start.1
  20.8 6.9 %all_gather.35 = bf16[512,128]{1,0:T(8,128)(2,1)} all-gather(bf16[128,128]{1,0:T(8,128)(2,1)} %param.14), channel_id=1, replica_groups=mesh['pb'=4,'ka'=8] {'pb'}, dimensions={0}, use_global_device_ids=true | all-gather | bytes 163840 | tf_op jit(solution)/shard_map/all_gather | solution.py:139
  28.1 2.7 collective-permute-start.2
  30.7 32.6 %all_gather.31 = f32[8,1024]{0,1:T(8,128)S(1)} all-gather(f32[8,128]{0,1:T(8,128)S(1)} %bitcast.125), channel_id=1, replica_groups=mesh['pb'=4,'ka'=8] {'ka'}, dimensions={1}, use_global_device_ids=true | all-gather | bytes 36864 | tf_op jit(solution)/shard_map/all_gather | solution.py:135
  63.5 5.1 %all-gather.2 = s32[4,1,128]{2,1,0:T(1,128)S(1)} all-gather(s32[1,1,128]{2,1,0:T(1,128)S(1)} %bitcast.128), channel_id=1, replica_groups=mesh['pb'=4,'ka'=8] {'pb'}, dimensions={0}, use_global_device_ids=true | all-gather | bytes 2560 | tf_op jit(solution)/shard_map/all_gather | solution.py:140
  68.5 5.0 %all-gather.3 = s32[4,1,128]{2,1,0:T(1,128)S(1)} all-gather(s32[1,1,128]{2,1,0:T(1,128)S(1)} %bitcast.130), channel_id=1, replica_groups=mesh['pb'=4,'ka'=8] {'pb'}, dimensions={0}, use_global_device_ids=true | all-gather | bytes 2560 | tf_op jit(solution)/shard_map/all_gather | solution.py:141
  73.6 17.0 %all-gather = s32[8,1,128]{2,1,0:T(1,128)S(1)} all-gather(s32[1,1,128]{2,1,0:T(1,128)S(1)} %bitcast.129), channel_id=1, replica_groups=mesh['pb'=4,'ka'=8] {'ka'}, dimensions={0}, use_global_device_ids=true | all-gather | bytes 4608 | tf_op jit(solution)/shard_map/all_gather | solution.py:130
  90.6 17.9 %all-gather.1 = s32[8,1,128]{2,1,0:T(1,128)S(1)} all-gather(s32[1,1,128]{2,1,0:T(1,128)S(1)} %bitcast.131), channel_id=1, replica_groups=mesh['pb'=4,'ka'=8] {'ka'}, dimensions={0}, use_global_device_ids=true | all-gather | bytes 4608 | tf_op jit(solution)/shard_map/all_gather | solution.py:131
  108.5 9.5 %all-gather.9.cloned.1.call-done = bf16[1024,1024]{1,0:T(8,128)(2,1)} async-done(((bf16[128,1024]{1,0:T(8,128)(2,1)}), bf16[1024,1024]{1,0:T(8,128)(2,1)}) %all-gather.9.cloned.1.call-update) | async-done | bytes 2097168 | tf_op jit(solution)/shard_map/all_gather | solution.py:129
  118.1 0.7 broadcast.67
  118.8 2.5 broadcast_in_dim.49.clone
  121.4 42.4 %while.52 = (s32[]{:T(128)}, f32[1024,1024]{1,0:T(8,128)}, f32[512,128]{1,0:T(8,128)}, f32[512,128]{1,0:T(8,128)S(1)}, s32[1024]{0:T(1024)S(1)}, /*index=5*/s32[...) while((s32[]{:T(128)}, f32[1024,1024]{1,0:T(8,128)}, ...), condition=%wide.region_4.5_spmd, body=%wide.region_1.4_spmd.sunk | while | flops 1354170368 | bytes 52825124 | solution.py:113
  122.7 2.8 constant_dynamic-slice_fusion.6
  125.5 11.9 %while.53 = (s32[]{:T(128)}, f32[512,1024]{0,1:T(8,128)S(1)}, f32[512,128]{1,0:T(8,128)}, f32[512,128]{1,0:T(8,128)S(1)}, bf16[512,128]{1,0:T(8,128)(2,1)S(1)}, ...) while((s32[]{:T(128)}, f32[512,1024]{0,1:T(8,128)S(1)}, ...), condition=%wide.region_3.3_spmd.clone, body=%wide.region_2.2_spmd.clone.sunk | while | flops 1354170368 | bytes 39578024 | solution.py:102
  125.9 0.7 fusion.79
  126.8 1.1 fusion.83
  127.9 1.6 fusion.80
  129.6 0.8 fusion.82
  131.8 0.7 fusion.79
  132.7 1.1 fusion.83
  133.9 1.6 fusion.80
  135.5 0.8 fusion.82
  137.4 1.9 copy.56
  139.3 3.2 %constant_dynamic-update-slice_fusion.2 = f32[1024,1024]{1,0:T(8,128)} fusion(f32[1024,1024]{1,0:T(8,128)} %get-tuple-element.913, f32[512,1024]{1,0:T(8,128)} %copy.56, s32[]{:T(128)S(6)} %select_n.89), kind=kLoop, calls=%fused_computation.38.clone.1 | loop fusion | bytes 4194308 | tf_op jit(solution)/shard_map/while/body/eval_jaxpr/dynamic_update_slice | solution.py:105
  143.9 2.8 constant_dynamic-slice_fusion.6
  146.7 11.9 %while.53 = (s32[]{:T(128)}, f32[512,1024]{0,1:T(8,128)S(1)}, f32[512,128]{1,0:T(8,128)}, f32[512,128]{1,0:T(8,128)S(1)}, bf16[512,128]{1,0:T(8,128)(2,1)S(1)}, ...) while((s32[]{:T(128)}, f32[512,1024]{0,1:T(8,128)S(1)}, ...), condition=%wide.region_3.3_spmd.clone, body=%wide.region_2.2_spmd.clone.sunk | while | flops 1354170368 | bytes 39578024 | solution.py:102
  147.9 1.1 fusion.83
  149.1 1.6 fusion.80
  150.8 0.8 fusion.82
  153.0 0.7 fusion.79
  153.9 1.1 fusion.83
  155.1 1.6 fusion.80
  156.7 0.8 fusion.82
  158.6 1.9 copy.56
  160.5 3.2 %constant_dynamic-update-slice_fusion.2 = f32[1024,1024]{1,0:T(8,128)} fusion(f32[1024,1024]{1,0:T(8,128)} %get-tuple-element.913, f32[512,1024]{1,0:T(8,128)} %copy.56, s32[]{:T(128)S(6)} %select_n.89), kind=kLoop, calls=%fused_computation.38.clone.1 | loop fusion | bytes 4194308 | tf_op jit(solution)/shard_map/while/body/eval_jaxpr/dynamic_update_slice | solution.py:105
  163.8 0.7 copy-done.1
  164.6 1.7 broadcast_multiply_fusion.1
  166.3 5.1 %broadcast_multiply_fusion = f32[1024,1024]{1,0:T(8,128)} fusion(f32[1024,1024]{1,0:T(8,128)} %get-tuple-element.501), kind=kLoop, calls=%fused_computation.43 | loop fusion | flops 1048576 | bytes 8388608 | tf_op jit(solution)/shard_map/mul | solution.py:155
  171.4 11.8 %reduce-scatter.8.cloned.1.call-done = f32[128,128]{1,0:T(8,128)} async-done(((f32[512,128]{1,0:T(8,128)}), f32[128,128]{1,0:T(8,128)}) %reduce-scatter.8.cloned.1.call-update) | async-done | bytes 65552 | tf_op jit(solution)/shard_map/reduce_scatter | solution.py:158
  183.3 1.5 convert_element_type.33
  184.7 21.5 %reduce-scatter.6.cloned.1.call-done = f32[128,128]{1,0:T(8,128)} async-done(((f32[512,128]{1,0:T(8,128)}), f32[128,128]{1,0:T(8,128)}) %reduce-scatter.6.cloned.1.call-update) | async-done | bytes 65552 | tf_op jit(solution)/shard_map/reduce_scatter | solution.py:157
  206.2 1.5 convert_element_type.32
  207.7 90.4 %reduce-scatter.4.cloned.1.call-done = f32[128,1024]{1,0:T(8,128)} async-done(((f32[1024,1024]{1,0:T(8,128)}), f32[128,1024]{1,0:T(8,128)}) %reduce-scatter.4.cloned.1.call-update) | async-done | bytes 524304 | tf_op jit(solution)/shard_map/reduce_scatter | solution.py:155
  298.1 1.8 convert_element_type.31
  (134 shorter events, 11.9 us)
Async XLA Ops:
  7.2 56.3 %copy-start.15 = (s32[128]{0:T(128)S(1)}, s32[128]{0:T(128)}, u32[]{:S(2)}) copy-start(s32[128]{0:T(128)} %param.18) | copy-start | bytes 1540
  7.2 61.3 %copy-start.16 = (s32[128]{0:T(128)S(1)}, s32[128]{0:T(128)}, u32[]{:S(2)}) copy-start(s32[128]{0:T(128)} %param.19) | copy-start | bytes 1540
  7.2 101.3 %all-gather.7.cloned.1.call-start = ((), (), s32[]{:S(2)}) async-start(), calls=%async_computation.3 | async-start | bytes 2359296 | tf_op jit(solution)/shard_map/all_gather | solution.py:128
  7.9 110.2 %all-gather.9.cloned.1.call-start = ((), (), s32[]{:S(2)}) async-start(), calls=%async_computation.4 | async-start | bytes 2359296 | tf_op jit(solution)/shard_map/all_gather | solution.py:129
  8.7 174.6 %reduce-scatter.8.cloned.1.call-start = ((), (), s32[]{:S(2)}) async-start(), calls=%async_computation.7 | async-start | bytes 327680 | tf_op jit(solution)/shard_map/reduce_scatter | solution.py:158
  8.7 9.8 %collective-permute-start = (f32[8,128]{1,0:T(8,128)}, f32[8,128]{1,0:T(8,128)S(1)}, u32[]{:S(2)}, u32[]{:S(2)}) collective-permute-start(f32[8,128]{1,0:T(8,128)} %param.17), channel_id=1, source_target_pairs={{0,1},{1,0},{2,3},{3,2},{4,5},{5,4},{6,7},{7,6},{8,9},{9,8},{10,11... | collective-permute-start | bytes 12296 | tf_op jit(solution)/shard_map/ppermute | solution.py:14
  19.3 8.8 %collective-permute-start.1 = (f32[8,256]{1,0:T(8,128)S(1)}, f32[8,256]{1,0:T(8,128)S(1)}, u32[]{:S(2)}, u32[]{:S(2)}) collective-permute-start(f32[8,256]{1,0:T(8,128)S(1)} %maximum_select_fusion.2), channel_id=1, source_target_pairs={{0,2},{1,3},{2,0},{3,1},{4,6},{5,7},{6,4},{7,5},{8,10},{9,11},{10,... | collective-permute-start | bytes 24584 | tf_op jit(solution)/shard_map/ppermute | solution.py:14
  28.1 80.4 %collective-permute-start.2 = (f32[8,512]{1,0:T(8,128)S(1)}, f32[8,512]{1,0:T(8,128)S(1)}, u32[]{:S(2)}, u32[]{:S(2)}) collective-permute-start(f32[8,512]{1,0:T(8,128)S(1)} %maximum_select_fusion.1), channel_id=1, source_target_pairs={{0,4},{1,5},{2,6},{3,7},{4,0},{5,1},{6,2},{7,3},{8,12},{9,13},{10,... | collective-permute-start | bytes 49160 | tf_op jit(solution)/shard_map/ppermute | solution.py:14
  121.4 1.3 copy-start.6
  121.4 1.3 copy-start.8
  121.4 1.3 copy-start.11
  125.5 1.2 copy-start
  125.5 1.2 copy-start.5
  126.8 1.2 copy-start.4
  126.8 1.2 copy-start.10
  127.9 1.6 copy-start.2
  130.3 1.1 copy-start.3
  131.5 1.2 copy-start
  131.5 1.2 copy-start.5
  132.7 1.2 copy-start.4
  132.7 1.2 copy-start.10
  133.9 1.6 copy-start.2
  136.3 1.1 copy-start.3
  137.4 5.1 %copy-start.14 = (s32[1024]{0:T(1024)S(1)}, s32[1024]{0:T(1024)}, u32[]{:S(2)}) copy-start(s32[1024]{0:T(1024)} %copy-done.13) | copy-start | bytes 12292 | tf_op jit(solution)/shard_map/while
  139.3 3.2 %copy-start.7 = (f32[8,1024]{1,0:T(8,128)S(1)}, f32[8,1024]{1,0:T(8,128)}, u32[]{:S(2)}) copy-start(f32[8,1024]{1,0:T(8,128)} %copy-done.6) | copy-start | bytes 98308 | tf_op jit(solution)/shard_map/while
  139.3 3.2 %copy-start.9 = (f32[8,1024]{1,0:T(8,128)S(1)}, f32[8,1024]{1,0:T(8,128)}, u32[]{:S(2)}) copy-start(f32[8,1024]{1,0:T(8,128)} %copy-done.8) | copy-start | bytes 98308 | tf_op jit(solution)/shard_map/while
  139.3 3.2 %copy-start.12 = (s32[1024]{0:T(1024)S(1)}, s32[1024]{0:T(1024)}, u32[]{:S(2)}) copy-start(s32[1024]{0:T(1024)} %copy-done.11) | copy-start | bytes 12292 | tf_op jit(solution)/shard_map/while
  142.6 1.3 copy-start.6
  142.6 1.3 copy-start.8
  142.6 1.3 copy-start.11
  146.7 1.2 copy-start
  146.7 1.2 copy-start.5
  147.9 1.2 copy-start.4
  147.9 1.2 copy-start.10
  149.1 1.6 copy-start.2
  151.5 1.1 copy-start.3
  152.7 1.2 copy-start
  152.7 1.2 copy-start.5
  153.9 1.2 copy-start.4
  153.9 1.2 copy-start.10
  155.1 1.6 copy-start.2
  157.5 1.1 copy-start.3
  158.6 5.2 %copy-start.14 = (s32[1024]{0:T(1024)S(1)}, s32[1024]{0:T(1024)}, u32[]{:S(2)}) copy-start(s32[1024]{0:T(1024)} %copy-done.13) | copy-start | bytes 12292 | tf_op jit(solution)/shard_map/while
  160.5 3.3 %copy-start.7 = (f32[8,1024]{1,0:T(8,128)S(1)}, f32[8,1024]{1,0:T(8,128)}, u32[]{:S(2)}) copy-start(f32[8,1024]{1,0:T(8,128)} %copy-done.6) | copy-start | bytes 98308 | tf_op jit(solution)/shard_map/while
  160.5 3.3 %copy-start.9 = (f32[8,1024]{1,0:T(8,128)S(1)}, f32[8,1024]{1,0:T(8,128)}, u32[]{:S(2)}) copy-start(f32[8,1024]{1,0:T(8,128)} %copy-done.8) | copy-start | bytes 98308 | tf_op jit(solution)/shard_map/while
  160.5 3.3 %copy-start.12 = (s32[1024]{0:T(1024)S(1)}, s32[1024]{0:T(1024)}, u32[]{:S(2)}) copy-start(s32[1024]{0:T(1024)} %copy-done.11) | copy-start | bytes 12292 | tf_op jit(solution)/shard_map/while
  164.5 41.7 %reduce-scatter.6.cloned.1.call-start = ((), (), s32[]{:S(2)}) async-start(), calls=%async_computation.6 | async-start | bytes 327680 | tf_op jit(solution)/shard_map/reduce_scatter | solution.py:157
  166.3 131.8 %reduce-scatter.4.cloned.1.call-start = ((), (), s32[]{:S(2)}) async-start(), calls=%async_computation.5 | async-start | bytes 4718592 | tf_op jit(solution)/shard_map/reduce_scatter | solution.py:155
  (3 other events, 1.9 us)
Sparse Core Ops, SparseCore 0:
  10.1 57.0 all-gather.6
  69.3 48.6 all-gather.8
  164.6 18.5 reduce-scatter.7
  186.1 20.0 reduce-scatter.5
  209.7 88.3 reduce-scatter.3
